TPU v7x, 256 devices: a whole 4x4x8 slice. The times are simulated.
256 devices in a mesh: gx: 16 (over z, core), gy: 4 (over x), gz: 4 (over y).
Axes of the slice: x: 4, y: 4, z: 8, core: 2. Of those that a mesh axis runs over, the one named last changes fastest.
Arguments:
- block_values: bfloat16 [4, 64, 4, 6, 128, 128], P('gy', 'gx', 'gz'), as said below
- block_cols: int32 [4, 64, 4, 6], P('gy', 'gx', 'gz'), may hold values from 0 to 63, as said below
Outputs:
- purified: float32 [2048, 32768], P(('gx', 'gy'), 'gz')
Inputs may be any that keep to these rules, and one draw needn't show every extreme that they name: block_cols[a, s, b, :] holds 6 distinct tile columns of panel b at which tile row a * 64 + s of P is nonzero; every tile column of a panel is listed by exactly 6 tile rows of each slab; the pattern is symmetric: tile (i, j) is listed exactly when tile (j, i) is. `block_values`: P is symmetric: the tile listed at (i, j) is the transpose of the tile listed at (j, i), and diagonal tiles are symmetric.
All inputs are finite; a program needn't handle non-finite values.
Results may differ from a plain program's by a relative error of at most 0.0033.
Values may be sent and summed in bfloat16 or wider, within the bound.
A program may use at most 128 MiB of HBM per device.

v0:
```python
import jax
import jax.numpy as jnp
from jax import lax
from jax.sharding import PartitionSpec as P

WIN = 1


def picked_2(x, axis, root):
    return lax.dynamic_index_in_dim(lax.all_gather(x, axis), root, 0, keepdims=False)


def in_blocks(x, dim, length):
    lengths = x.shape
    tiles = x.reshape(*lengths[:dim], length, lengths[dim] // length, *lengths[dim + 1 :])
    return jnp.moveaxis(tiles, dim, 0)


def sent_and_summed(x, axis, dim):
    tiles = in_blocks(x, dim, lax.axis_size(axis))
    arrived = lax.all_to_all(tiles, axis, split_axis=0, concat_axis=0, tiled=True)
    return arrived.astype(jnp.float32).sum(axis=0)


def densify(left_tiles, left_columns, slab_tiles):
    onehot = (
        left_columns[:, :, None] == jnp.arange(slab_tiles, dtype=jnp.int32)[None, None, :]
    ).astype(jnp.bfloat16)
    densified = jnp.einsum("wkj,wkyx->wyjx", onehot, left_tiles, preferred_element_type=jnp.float32)
    tile_size = left_tiles.shape[2]
    return densified.astype(jnp.bfloat16).reshape(
        left_tiles.shape[0] * tile_size, slab_tiles, tile_size
    )


def product_one(left_panel, panel_tiles, panel_columns):
    summed = jnp.zeros(
        (left_panel.shape[0], panel_tiles.shape[0], panel_tiles.shape[2]), jnp.float32
    )
    for column_slot in range(panel_tiles.shape[1]):
        picked = jnp.take(left_panel, panel_columns[:, column_slot], axis=1)
        summed = summed + jnp.einsum(
            "rix,iyx->riy", picked, panel_tiles[:, column_slot], preferred_element_type=jnp.float32
        )
    return summed


def product_two(rounded, panel_tiles, panel_columns, panel_width):
    summed = jnp.zeros((rounded.shape[0], panel_width, panel_tiles.shape[3]), jnp.float32)
    for column_slot in range(panel_tiles.shape[1]):
        product = jnp.einsum(
            "rix,ixy->riy", rounded, panel_tiles[:, column_slot], preferred_element_type=jnp.float32
        )
        summed = summed.at[:, panel_columns[:, column_slot], :].add(product)
    return summed


def local(block_values, block_cols):
    tiles_here = block_values[0, :, 0]
    columns_here = block_cols[0, :, 0]
    tile_size = tiles_here.shape[2]
    slab_tiles = tiles_here.shape[0] * lax.axis_size("gx")
    left_tiles, left_columns = (
        picked_2(tiles_here[:WIN], "gy", 0),
        picked_2(columns_here[:WIN], "gy", 0),
    )
    left_panel = densify(left_tiles, left_columns, slab_tiles)
    height = left_panel.shape[0]
    on_diagonal = (lax.axis_index("gy") == lax.axis_index("gz")).astype(jnp.float32)
    panel_tiles, panel_columns = (
        lax.all_gather(tiles_here, "gx", axis=0, tiled=True),
        lax.all_gather(columns_here, "gx", axis=0, tiled=True),
    )
    partial_square = product_one(left_panel, panel_tiles, panel_columns)
    partial_square = partial_square.reshape(height, slab_tiles * tile_size)
    square = lax.psum(partial_square, "gz")
    square_low = square.astype(jnp.bfloat16).reshape(height, slab_tiles, tile_size)
    applied = product_two(square_low, panel_tiles, panel_columns, slab_tiles).reshape(
        height // lax.axis_size("gy") * lax.axis_size("gy"), slab_tiles * tile_size
    )
    return sent_and_summed(
        (3.0 * on_diagonal * square - 2.0 * applied).astype(jnp.bfloat16), "gy", 0
    )


def solution(mesh):
    in_specs = (P("gy", "gx", "gz", None, None, None), P("gy", "gx", "gz", None))
    out_specs = P(("gx", "gy"), "gz")
    return jax.shard_map(local, mesh=mesh, in_specs=in_specs, out_specs=out_specs, check_vma=False)
```

profile of v0, /device:TPU:32, one launch (start us, length us, event | category | flops | bytes accessed | tf_op | source)
XLA Modules:
  0.0 381.8 jit_solution(5912386459244780532)
XLA Ops:
  6.5 0.0 all-gather.6.cloned.1.call-start
  6.5 2.2 copy.30
  8.7 0.0 all-gather.6.cloned.1.call-update
  8.7 0.0 all-reduce.2.cloned.1.call-start
  8.8 9.7 %all-gather = s32[4,1,1,6]{3,2,1,0:T(1,128)S(1)} all-gather(s32[1,1,1,6]{3,2,1,0:T(1,128)S(1)} %slice-done.4), channel_id=2, replica_groups=mesh['gx'=16,'gy'=4,'gz'=4] {'gy'}, dimensions={0}, use_global_device_ids=true | all-gather | bytes 120 | tf_op jit(solution)/shard_map/all_gather | solution.py:10
  18.5 13.3 %all-gather.1 = bf16[4,1,1,6,128,128]{5,4,3,2,1,0:T(8,128)(2,1)S(1)} all-gather(bf16[1,1,1,6,128,128]{5,4,3,2,1,0:T(8,128)(2,1)S(1)} %slice-done.3), channel_id=3, replica_groups=mesh['gx'=16,'gy'=4,'gz'=4] {'gy'}, dimensions={0}, use_global_device_ids=true | all-gather | bytes 983040 | tf_op jit(solution)/shard_map/all_gather | solution.py:10
  31.8 0.8 convert_bitcast_fusion
  32.7 0.0 copy-start.5
  32.7 1.4 copy.29
  34.0 0.0 copy-done.5
  34.1 18.6 %all-gather.2 = s32[1,64,1,6]{3,2,0,1:T(1,128)S(1)} all-gather(s32[1,4,1,6]{3,2,0,1:T(1,128)S(1)} %bitcast.101), channel_id=4, replica_groups=mesh['gx'=16,'gy'=4,'gz'=4] {'gx'}, dimensions={1}, use_global_device_ids=true | all-gather | bytes 1632 | tf_op jit(solution)/shard_map/all_gather | solution.py:72
  52.7 0.4 fusion.41
  53.1 2.2 gather_fusion
  55.3 2.1 gather_fusion.4
  57.4 2.2 gather_fusion.3
  59.6 2.1 gather_fusion.2
  61.7 2.2 gather_fusion.1
  63.9 2.1 gather_fusion.5
  66.1 19.6 %all-gather.6.cloned.1.call-done = bf16[1,64,1,6,128,128]{5,4,1,3,2,0:T(8,128)(2,1)} async-done(((bf16[1,4,1,6,128,128]{5,4,1,3,2,0:T(8,128)(2,1)}), bf16[1,64,1,6,128,128]{5,4,1,3,2,0:T(8,128)(2,1)}) %all-gather.6.cloned.1.call-update) | async-done | bytes 12582928 | tf_op jit(solution)/shard_map/all_gather | solution.py:71
  85.7 6.2 %fusion.10 = f32[64,128,128]{1,2,0:T(8,128)} fusion(bf16[64,128,128]{2,1,0:T(8,128)(2,1)} %gather_fusion, pred[64]{0:T(512)(128)(4,1)S(1)} %get-tuple-element.29, bf16[64,6,128,128]{3,2,0,1:T(8,128)(2,1)} %bitcast.84), kind=kOutput, calls=%fused_computation.31 | convolution fusion | flops 269484032 | bytes 8388672 | tf_op jit(solution)/shard_map/rix,iyx->riy/dot_general | solution.py:42
  91.8 6.0 %fusion.2 = f32[64,128,128]{1,2,0:T(8,128)} fusion(bf16[64,128,128]{2,1,0:T(8,128)(2,1)} %gather_fusion.4, pred[64]{0:T(512)(128)(4,1)S(1)} %get-tuple-element.25, bf16[64,6,128,128]{3,2,0,1:T(8,128)(2,1)} %bitcast.85), kind=kOutput, calls=%fused_computation.23 | convolution fusion | flops 269484032 | bytes 8388672 | tf_op jit(solution)/shard_map/rix,iyx->riy/dot_general | solution.py:42
  97.8 3.6 fusion.4
  101.5 3.6 fusion.6
  105.1 3.6 fusion.8
  108.7 10.1 %add_add_fusion = f32[64,128,128]{1,2,0:T(8,128)} fusion(f32[64,128,128]{1,2,0:T(8,128)} %fusion.2, f32[64,128,128]{1,2,0:T(8,128)} %fusion.4, f32[64,128,128]{1,2,0:T(8,128)} %fusion.6, f32[64,128,128]{1,2,0:T(8,128)} %fusion.10, f32[64,128,128]{1,2,0:T(8,128)} %fusion.8, bf16[64,128,128]{2,1,0:T(8,128)(2,1)S(1)} %copy-done.4, ...), kind=kOutput, calls=%fused_computation.15 | convolution fusion | flops 274726912 | bytes 29360640 | tf_op jit(solution)/shard_map/rix,iyx->riy/dot_general | solution.py:42
  118.8 0.0 all-reduce.2.cloned.1.call-update
  118.8 98.5 %all-reduce.2.cloned.1.call-done = f32[128,8192]{0,1:T(8,128)} async-done(((f32[128,8192]{0,1:T(8,128)}), f32[128,8192]{0,1:T(8,128)}) %all-reduce.2.cloned.1.call-update) | async-done | bytes 4194320 | tf_op jit(solution)/shard_map/psum | solution.py:76
  217.4 2.5 convert_element_type.27
  219.9 0.0 slice-start.1
  219.9 4.6 %fusion.24 = f32[64,128,128]{2,1,0:T(8,128)} fusion(bf16[128,64,128]{0,2,1:T(8,128)(2,1)S(1)} %bitcast.78, bf16[64,6,128,128]{3,2,0,1:T(8,128)(2,1)} %bitcast.86), kind=kOutput, calls=%fused_computation.47 | convolution fusion | flops 268435456 | bytes 8388608 | tf_op jit(solution)/shard_map/rix,ixy->riy/dot_general | solution.py:51
  224.5 4.6 %fusion.25 = f32[64,128,128]{2,1,0:T(8,128)} fusion(bf16[128,64,128]{0,2,1:T(8,128)(2,1)S(1)} %bitcast.79, bf16[64,6,128,128]{3,2,0,1:T(8,128)(2,1)} %bitcast.87), kind=kOutput, calls=%fused_computation.48 | convolution fusion | flops 268435456 | bytes 8388608 | tf_op jit(solution)/shard_map/rix,ixy->riy/dot_general | solution.py:51
  229.1 2.8 fusion.26
  231.9 2.8 fusion.27
  234.7 2.8 fusion.28
  237.5 2.8 fusion.29
  240.3 2.5 broadcast_in_dim.11
  242.8 13.7 %scatter_fusion = f32[128,64,128]{2,0,1:T(8,128)} fusion(f32[128,64,128]{2,0,1:T(8,128)} %broadcast_in_dim.11, s32[64]{0:T(128)S(1)} %get-tuple-element.7, f32[64,128,128]{2,1,0:T(8,128)} %fusion.24), kind=kCustom, calls=%fused_computation.6 | custom fusion | flops 1048576 | bytes 12583168 | tf_op jit(solution)/shard_map/scatter-add | solution.py:54
  256.5 13.7 %scatter_fusion.1 = f32[128,64,128]{2,0,1:T(8,128)} fusion(f32[128,64,128]{2,0,1:T(8,128)} %scatter_fusion, s32[64]{0:T(128)S(1)} %get-tuple-element.8, f32[64,128,128]{2,1,0:T(8,128)} %fusion.25), kind=kCustom, calls=%fused_computation.7 | custom fusion | flops 1048576 | bytes 12583168 | tf_op jit(solution)/shard_map/scatter-add | solution.py:54
  270.2 13.7 %scatter_fusion.2 = f32[128,64,128]{2,0,1:T(8,128)} fusion(f32[128,64,128]{2,0,1:T(8,128)} %scatter_fusion.1, s32[64]{0:T(128)S(1)} %get-tuple-element.9, f32[64,128,128]{2,1,0:T(8,128)} %fusion.26), kind=kCustom, calls=%fused_computation.8 | custom fusion | flops 1048576 | bytes 12583168 | tf_op jit(solution)/shard_map/scatter-add | solution.py:54
  283.9 13.6 %scatter_fusion.3 = f32[128,64,128]{2,0,1:T(8,128)} fusion(f32[128,64,128]{2,0,1:T(8,128)} %scatter_fusion.2, s32[64]{0:T(128)S(1)} %get-tuple-element.10, f32[64,128,128]{2,1,0:T(8,128)} %fusion.27), kind=kCustom, calls=%fused_computation.9 | custom fusion | flops 1048576 | bytes 12583168 | tf_op jit(solution)/shard_map/scatter-add | solution.py:54
  297.5 13.7 %scatter_fusion.4 = f32[128,64,128]{2,0,1:T(8,128)} fusion(f32[128,64,128]{2,0,1:T(8,128)} %scatter_fusion.3, s32[64]{0:T(128)S(1)} %get-tuple-element.11, f32[64,128,128]{2,1,0:T(8,128)} %fusion.28), kind=kCustom, calls=%fused_computation.10 | custom fusion | flops 1048576 | bytes 12583168 | tf_op jit(solution)/shard_map/scatter-add | solution.py:54
  311.1 13.6 %scatter_fusion.5 = f32[128,64,128]{2,0,1:T(8,128)} fusion(f32[128,64,128]{2,0,1:T(8,128)} %scatter_fusion.4, s32[64]{0:T(128)S(1)} %get-tuple-element.6, f32[64,128,128]{2,1,0:T(8,128)} %fusion.29), kind=kCustom, calls=%fused_computation.11 | custom fusion | flops 1048576 | bytes 12583168 | tf_op jit(solution)/shard_map/scatter-add | solution.py:54
  324.8 4.7 %broadcast_multiply_fusion = f32[128,64,128]{2,0,1:T(8,128)} fusion(f32[128,64,128]{2,0,1:T(8,128)} %scatter_fusion.5), kind=kLoop, calls=%fused_computation.39 | loop fusion | flops 1048576 | bytes 8388608 | tf_op jit(solution)/shard_map/mul | solution.py:82
  329.5 5.6 %copy.42 = f32[128,64,128]{0,2,1:T(8,128)} copy(f32[128,64,128]{2,0,1:T(8,128)} %broadcast_multiply_fusion) | data formatting | bytes 8388608 | tf_op jit(solution)/shard_map/mul | solution.py:82
  335.1 5.2 %fusion = bf16[128,8192]{0,1:T(8,128)(2,1)} fusion(f32[128,64,128]{0,2,1:T(8,128)} %copy.42, f32[128,8192]{0,1:T(8,128)} %all-reduce.2.cloned.1.call-done, f32[]{:T(128)S(6)} %mul_shard_map.3), kind=kLoop, calls=%fused_computation.13 | loop fusion | flops 3145728 | bytes 10485764 | tf_op jit(solution)/shard_map/convert_element_type | solution.py:82
  340.3 2.9 copy.43
  343.3 30.4 %all_to_all.5 = bf16[4,32,8192]{2,1,0:T(8,128)(2,1)S(1)} all-to-all(bf16[4,32,8192]{2,1,0:T(8,128)(2,1)S(1)} %bitcast.99), channel_id=1, replica_groups=mesh['gx'=16,'gy'=4,'gz'=4] {'gy'}, dimensions={0} | all-to-all | bytes 4194304 | tf_op jit(solution)/shard_map/all_to_all | solution.py:21
  373.6 1.3 convert_reduce_fusion
  (34 shorter events, 0.1 us)
Async XLA Ops:
  6.5 12.0 %slice-start.3 = ((bf16[1,4,1,6,128,128]{5,4,3,2,1,0:T(8,128)(2,1)}), bf16[1,1,1,6,128,128]{5,4,3,2,1,0:T(8,128)(2,1)S(1)}, s32[]{:S(2)}) async-start(bf16[1,4,1,6,128,128]{5,4,3,2,1,0:T(8,128)(2,1)} %param.4), calls=%async_computation.6 | async-start | bytes 393216 | tf_op jit(solution)/shard_map/slice | solution.py:64
  6.5 2.2 slice-start.4
  6.5 79.1 %all-gather.6.cloned.1.call-start = ((), (), s32[]{:S(2)}) async-start(), calls=%async_computation.2 | async-start | bytes 13369344 | tf_op jit(solution)/shard_map/all_gather | solution.py:71
  8.7 208.6 %all-reduce.2.cloned.1.call-start = ((), (), s32[]{:S(2)}) async-start(), calls=%async_computation.1 | async-start | bytes 8388608 | tf_op jit(solution)/shard_map/psum | solution.py:76
  32.7 1.4 copy-start.5
  85.7 12.2 %copy-start = (bf16[1,64,1,6,128,128]{5,4,1,3,2,0:T(8,128)(2,1)S(1)}, bf16[1,64,1,6,128,128]{5,4,1,3,2,0:T(8,128)(2,1)}, u32[]{:S(2)}) copy-start(bf16[1,64,1,6,128,128]{5,4,1,3,2,0:T(8,128)(2,1)} %all-gather.6.cloned.1.call-done) | copy-start | bytes 37748740
  91.8 6.0 %copy-start.1 = (bf16[64,128,128]{2,1,0:T(8,128)(2,1)S(1)}, bf16[64,128,128]{2,1,0:T(8,128)(2,1)}, u32[]{:S(2)}) copy-start(bf16[64,128,128]{2,1,0:T(8,128)(2,1)} %gather_fusion.3) | copy-start | bytes 6291460
  97.8 3.6 copy-start.2
  101.5 3.6 copy-start.3
  105.1 3.6 copy-start.4
  217.4 11.7 %slice-start = ((s8[12582912]{0:T(1024)(128)(4,1)}), s8[4194304]{0:T(1024)(128)(4,1)S(1)}, s32[]{:S(2)}) async-start(s8[12582912]{0:T(1024)(128)(4,1)} %bitcast.92), calls=%async_computation.3 | async-start | bytes 8388608
  219.9 9.2 %slice-start.1 = ((s8[12582912]{0:T(1024)(128)(4,1)}), s8[4194304]{0:T(1024)(128)(4,1)S(1)}, s32[]{:S(2)}) async-start(s8[12582912]{0:T(1024)(128)(4,1)} %bitcast.92), calls=%async_computation.4 | async-start | bytes 8388608
  224.5 4.6 %slice-start.2 = ((s8[12582912]{0:T(1024)(128)(4,1)}), s8[4194304]{0:T(1024)(128)(4,1)S(1)}, s32[]{:S(2)}) async-start(s8[12582912]{0:T(1024)(128)(4,1)} %bitcast.92), calls=%async_computation.5 | async-start | bytes 8388608
Sparse Core Ops, SparseCore 0:
  9.2 76.4 all-gather.5
  118.9 98.3 all-reduce.1
where the time goes:
time: 383 us; the launch traced here: 382 us
  waiting for transfers between devices  118 us (31%)
  other arithmetic  96.3 us (25%)
  blocking collectives  72 us (19%)
  matrix products  54.3 us (14%)
  local copies, waits for them, and re-layouts  27.4 us (7%)
  between operations  13.5 us (4%)
    psum x1, waiting for transfers between devices, local(): square = lax.psum(partial_square, 'gz')  98.5 us
    scatter-add x6, other arithmetic, product_two(): summed = summed.at[:, panel_columns[:, column_slot], :].add(product)  82 us
    dot_general x6, matrix products, product_one(): jnp.einsum('rix,iyx->riy', picked, panel_tiles[:, column_slot], preferred...  33.1 us
    all_to_all x1, blocking collectives, sent_and_summed(): lax.all_to_all(tiles, axis, split_axis=0, concat_axis=0, tiled=True)  30.4 us
    all_gather x2, blocking collectives, picked_2(): lax.all_gather(x, axis)  23 us
    dot_general x6, matrix products, product_two(): jnp.einsum('rix,ixy->riy', rounded, panel_tiles[:, column_slot], preferre...  20.4 us
    all_gather x1, waiting for transfers between devices, local(): lax.all_gather(tiles_here, 'gx', axis=0, tiled=True)  19.6 us
    all_gather x1, blocking collectives, local(): lax.all_gather(columns_here, 'gx', axis=0, tiled=True)  18.6 us
  transfers between devices with their start and end apart: 2, of which 2 were waited for; matrix products, arithmetic and copies ran while one was open for 4% of the time, Pallas kernels for 0%

commit v1 on v0

--- a/solution.py
+++ b/solution.py
@@ -73,7 +73,8 @@
     )
     partial_square = product_one(left_panel, panel_tiles, panel_columns)
     partial_square = partial_square.reshape(height, slab_tiles * tile_size)
-    square = lax.psum(partial_square, "gz")
+    parts = lax.all_gather(partial_square, "gz")
+    square = jnp.sum(parts, axis=0)
     square_low = square.astype(jnp.bfloat16).reshape(height, slab_tiles, tile_size)
     applied = product_two(square_low, panel_tiles, panel_columns, slab_tiles).reshape(
         height // lax.axis_size("gy") * lax.axis_size("gy"), slab_tiles * tile_size

time: 383 us -> 470 us (1.23)
  waiting for transfers between devices: 118 us -> 175 us
  local copies, waits for them, and re-layouts: 27.4 us -> 46.7 us
  other arithmetic: 96.3 us -> 106 us
    all_gather x0 -> x1, waiting for transfers between devices: none -> 157 us  [local(): parts = lax.all_gather(partial_square, 'gz')]
    psum x1 -> x0, waiting for transfers between devices: 98.5 us -> none  [local(): square = lax.psum(partial_square, 'gz')]
    reduce_sum x0 -> x1, other arithmetic: none -> 9.45 us  [local(): square = jnp.sum(parts, axis=0)]
    mul x0 -> x1, local copies, waits for them, and re-layouts: none -> 5.65 us  [local(): 3.0 * on_diagonal * square - 2.0 * applied]
    another operation x0 -> x1, local copies, waits for them, and re-layouts: none -> 5.6 us  [local(): parts = lax.all_gather(partial_square, 'gz')]
    unnamed x19 -> x20, local copies, waits for them, and re-layouts: 2.19 us -> 7.73 us
where the time goes in v1:
time: 470 us; the launch traced here: 468 us
  waiting for transfers between devices  175 us (37%)
  other arithmetic  106 us (23%)
  blocking collectives  71.8 us (15%)
  matrix products  54.4 us (12%)
  local copies, waits for them, and re-layouts  46.7 us (10%)
  between operations  13.5 us (3%)
    all_gather x1, waiting for transfers between devices, local(): parts = lax.all_gather(partial_square, 'gz')  157 us
    scatter-add x6, other arithmetic, product_two(): summed = summed.at[:, panel_columns[:, column_slot], :].add(product)  82.2 us
    dot_general x6, matrix products, product_one(): jnp.einsum('rix,iyx->riy', picked, panel_tiles[:, column_slot], preferred...  33.3 us
    all_to_all x1, blocking collectives, sent_and_summed(): lax.all_to_all(tiles, axis, split_axis=0, concat_axis=0, tiled=True)  30.2 us
    all_gather x2, blocking collectives, picked_2(): lax.all_gather(x, axis)  23 us
    dot_general x6, matrix products, product_two(): jnp.einsum('rix,ixy->riy', rounded, panel_tiles[:, column_slot], preferre...  20.3 us
    all_gather x1, blocking collectives, local(): lax.all_gather(columns_here, 'gx', axis=0, tiled=True)  18.6 us
    all_gather x1, waiting for transfers between devices, local(): lax.all_gather(tiles_here, 'gx', axis=0, tiled=True)  18 us
  transfers between devices with their start and end apart: 2, of which 2 were waited for; matrix products, arithmetic and copies ran while one was open for 4% of the time, Pallas kernels for 0%

profile of v1, /device:TPU:32, one launch (start us, length us, event | category | flops | bytes accessed | tf_op | source)
XLA Modules:
  0.0 467.9 jit_solution(3969880518924371694)
XLA Ops:
  6.5 2.1 copy.46
  8.7 0.0 all-gather.7.cloned.1.call-start
  8.7 0.7 slice.58
  9.4 9.7 %all-gather = s32[4,1,1,6]{3,2,1,0:T(1,128)S(1)} all-gather(s32[1,1,1,6]{3,2,1,0:T(1,128)S(1)} %slice.58), channel_id=2, replica_groups=mesh['gx'=16,'gy'=4,'gz'=4] {'gy'}, dimensions={0}, use_global_device_ids=true | all-gather | bytes 120 | tf_op jit(solution)/shard_map/all_gather | solution.py:10
  19.1 0.9 slice.59
  20.0 13.3 %all-gather.1 = bf16[4,1,1,6,128,128]{5,4,3,2,1,0:T(8,128)(2,1)S(1)} all-gather(bf16[1,1,1,6,128,128]{5,4,3,2,1,0:T(8,128)(2,1)S(1)} %slice.59), channel_id=3, replica_groups=mesh['gx'=16,'gy'=4,'gz'=4] {'gy'}, dimensions={0}, use_global_device_ids=true | all-gather | bytes 983040 | tf_op jit(solution)/shard_map/all_gather | solution.py:10
  33.4 0.8 convert_bitcast_fusion
  34.2 1.4 copy.45
  35.6 18.6 %all-gather.2 = s32[1,64,1,6]{3,2,0,1:T(1,128)S(1)} all-gather(s32[1,4,1,6]{3,2,0,1:T(1,128)S(1)} %bitcast.97), channel_id=4, replica_groups=mesh['gx'=16,'gy'=4,'gz'=4] {'gx'}, dimensions={1}, use_global_device_ids=true | all-gather | bytes 1632 | tf_op jit(solution)/shard_map/all_gather | solution.py:72
  54.2 0.4 fusion.40
  54.6 2.2 gather_fusion.3
  56.8 2.2 gather_fusion.2
  58.9 2.2 gather_fusion.1
  61.1 2.2 gather_fusion
  63.3 2.1 gather_fusion.4
  65.4 2.1 gather_fusion.5
  67.6 18.0 %all-gather.9.cloned.1.call-done = bf16[1,64,1,6,128,128]{5,4,1,3,2,0:T(8,128)(2,1)} async-done(((bf16[1,4,1,6,128,128]{5,4,1,3,2,0:T(8,128)(2,1)}), bf16[1,64,1,6,128,128]{5,4,1,3,2,0:T(8,128)(2,1)}) %all-gather.9.cloned.1.call-update) | async-done | bytes 12582928 | tf_op jit(solution)/shard_map/all_gather | solution.py:71
  85.7 6.2 %fusion.3 = f32[64,128,128]{1,2,0:T(8,128)} fusion(bf16[64,128,128]{2,1,0:T(8,128)(2,1)} %gather_fusion.3, pred[64]{0:T(512)(128)(4,1)S(1)} %get-tuple-element.28, bf16[64,6,128,128]{3,2,0,1:T(8,128)(2,1)} %bitcast.80), kind=kOutput, calls=%fused_computation.24 | convolution fusion | flops 269484032 | bytes 8388672 | tf_op jit(solution)/shard_map/rix,iyx->riy/dot_general | solution.py:42
  91.8 6.0 %fusion.5 = f32[64,128,128]{1,2,0:T(8,128)} fusion(bf16[64,128,128]{2,1,0:T(8,128)(2,1)} %gather_fusion.2, pred[64]{0:T(512)(128)(4,1)S(1)} %get-tuple-element.29, bf16[64,6,128,128]{3,2,0,1:T(8,128)(2,1)} %bitcast.81), kind=kOutput, calls=%fused_computation.26 | convolution fusion | flops 269484032 | bytes 8388672 | tf_op jit(solution)/shard_map/rix,iyx->riy/dot_general | solution.py:42
  97.8 3.7 fusion.7
  101.5 3.6 fusion.9
  105.1 3.7 fusion.1
  108.9 10.2 %add_add_fusion = f32[64,128,128]{1,2,0:T(8,128)} fusion(f32[64,128,128]{1,2,0:T(8,128)} %fusion.1, f32[64,128,128]{1,2,0:T(8,128)} %fusion.3, f32[64,128,128]{1,2,0:T(8,128)} %fusion.5, f32[64,128,128]{1,2,0:T(8,128)} %fusion.9, f32[64,128,128]{1,2,0:T(8,128)} %fusion.7, bf16[64,128,128]{2,1,0:T(8,128)(2,1)S(1)} %copy-done.4, ...), kind=kOutput, calls=%fused_computation.14 | convolution fusion | flops 274726912 | bytes 29360640 | tf_op jit(solution)/shard_map/rix,iyx->riy/dot_general | solution.py:42
  119.0 5.6 %copy.52 = f32[1,128,8192]{2,1,0:T(8,128)} copy(f32[1,128,8192]{1,2,0:T(8,128)} %bitcast.95) | data formatting | bytes 8388608 | tf_op jit(solution)/shard_map/all_gather;reshape | solution.py:76
  124.7 157.2 %all-gather.7.cloned.1.call-done = f32[4,128,8192]{2,1,0:T(8,128)} async-done(((f32[1,128,8192]{2,1,0:T(8,128)}), f32[4,128,8192]{2,1,0:T(8,128)}) %all-gather.7.cloned.1.call-update) | async-done | bytes 16777232 | tf_op jit(solution)/shard_map/all_gather | solution.py:76
  281.9 9.5 %reduce_sum.18 = f32[128,8192]{1,0:T(8,128)} reduce(f32[4,128,8192]{2,1,0:T(8,128)} %all-gather.7.cloned.1.call-done, f32[]{:T(128)} %constant.20.clone.1), dimensions={0}, to_apply=%region_0.2 | reduce | flops 3145728 | bytes 20971524 | tf_op jit(solution)/shard_map/reduce_sum | solution.py:77
  291.3 5.6 %copy.68 = f32[128,8192]{0,1:T(8,128)} copy(f32[128,8192]{1,0:T(8,128)} %reduce_sum.18) | data formatting | bytes 8388608
  296.9 6.3 %fusion.50 = (bf16[128,8192]{0,1:T(8,128)(2,1)S(1)}, f32[128,8192]{0,1:T(8,128)}) fusion(f32[128,8192]{0,1:T(8,128)} %copy.68, f32[]{:T(128)S(6)} %mul_shard_map.3), kind=kLoop, calls=%fused_computation.106 | loop fusion | flops 2097152 | bytes 10485764 | tf_op jit(solution)/shard_map/convert_element_type | solution.py:78
  303.2 4.6 fusion.23
  307.8 4.4 fusion.24
  312.2 2.8 fusion.25
  315.1 2.8 fusion.26
  317.9 2.8 fusion.27
  320.7 2.8 fusion.28
  323.5 2.4 broadcast_in_dim.11
  326.0 13.7 %scatter_fusion = f32[128,64,128]{2,0,1:T(8,128)} fusion(f32[128,64,128]{2,0,1:T(8,128)} %broadcast_in_dim.11, s32[64]{0:T(128)S(1)} %get-tuple-element.7, f32[64,128,128]{2,1,0:T(8,128)} %fusion.23), kind=kCustom, calls=%fused_computation.6 | custom fusion | flops 1048576 | bytes 12583168 | tf_op jit(solution)/shard_map/scatter-add | solution.py:54
  339.7 13.7 %scatter_fusion.1 = f32[128,64,128]{2,0,1:T(8,128)} fusion(f32[128,64,128]{2,0,1:T(8,128)} %scatter_fusion, s32[64]{0:T(128)S(1)} %get-tuple-element.8, f32[64,128,128]{2,1,0:T(8,128)} %fusion.24), kind=kCustom, calls=%fused_computation.7 | custom fusion | flops 1048576 | bytes 12583168 | tf_op jit(solution)/shard_map/scatter-add | solution.py:54
  353.3 13.7 %scatter_fusion.2 = f32[128,64,128]{2,0,1:T(8,128)} fusion(f32[128,64,128]{2,0,1:T(8,128)} %scatter_fusion.1, s32[64]{0:T(128)S(1)} %get-tuple-element.9, f32[64,128,128]{2,1,0:T(8,128)} %fusion.25), kind=kCustom, calls=%fused_computation.8 | custom fusion | flops 1048576 | bytes 12583168 | tf_op jit(solution)/shard_map/scatter-add | solution.py:54
  367.0 13.9 %scatter_fusion.3 = f32[128,64,128]{2,0,1:T(8,128)} fusion(f32[128,64,128]{2,0,1:T(8,128)} %scatter_fusion.2, s32[64]{0:T(128)S(1)} %get-tuple-element.10, f32[64,128,128]{2,1,0:T(8,128)} %fusion.26), kind=kCustom, calls=%fused_computation.9 | custom fusion | flops 1048576 | bytes 12583168 | tf_op jit(solution)/shard_map/scatter-add | solution.py:54
  380.9 13.7 %scatter_fusion.4 = f32[128,64,128]{2,0,1:T(8,128)} fusion(f32[128,64,128]{2,0,1:T(8,128)} %scatter_fusion.3, s32[64]{0:T(128)S(1)} %get-tuple-element.11, f32[64,128,128]{2,1,0:T(8,128)} %fusion.27), kind=kCustom, calls=%fused_computation.10 | custom fusion | flops 1048576 | bytes 12583168 | tf_op jit(solution)/shard_map/scatter-add | solution.py:54
  394.6 13.6 %scatter_fusion.5 = f32[128,64,128]{2,0,1:T(8,128)} fusion(f32[128,64,128]{2,0,1:T(8,128)} %scatter_fusion.4, s32[64]{0:T(128)S(1)} %get-tuple-element.6, f32[64,128,128]{2,1,0:T(8,128)} %fusion.28), kind=kCustom, calls=%fused_computation.11 | custom fusion | flops 1048576 | bytes 12583168 | tf_op jit(solution)/shard_map/scatter-add | solution.py:54
  408.2 2.5 broadcast_multiply_fusion
  410.7 4.4 copy.61
  415.1 4.9 %mul.25 = f32[4,32,8192]{2,1,0:T(8,128)} reshape(f32[128,64,128]{2,1,0:T(8,128)} %copy.61) | data formatting | bytes 8388608 | tf_op jit(solution)/shard_map/mul | solution.py:83
  420.1 5.6 %copy.54 = f32[128,8192]{1,0:T(8,128)} copy(f32[128,8192]{0,1:T(8,128)} %get-tuple-element.19) | data formatting | bytes 8388608 | tf_op jit(solution)/shard_map/mul | solution.py:83
  425.7 3.9 subtract_convert_fusion
  429.6 30.2 %all_to_all.5 = bf16[4,32,8192]{2,1,0:T(8,128)(2,1)S(1)} all-to-all(bf16[4,32,8192]{2,1,0:T(8,128)(2,1)S(1)} %subtract_convert_fusion), channel_id=1, replica_groups=mesh['gx'=16,'gy'=4,'gz'=4] {'gy'}, dimensions={0} | all-to-all | bytes 4194304 | tf_op jit(solution)/shard_map/all_to_all | solution.py:21
  459.8 1.3 convert_reduce_fusion
  (36 shorter events, 0.2 us)
Async XLA Ops:
  6.5 79.1 %all-gather.9.cloned.1.call-start = ((), (), s32[]{:S(2)}) async-start(), calls=%async_computation.2 | async-start | bytes 13369344 | tf_op jit(solution)/shard_map/all_gather | solution.py:71
  8.6 26.9 %copy-start.5 = (s32[1,4,1,6]{3,2,1,0:T(1,128)S(1)}, s32[1,4,1,6]{3,2,1,0:T(1,128)}, u32[]{:S(2)}) copy-start(s32[1,4,1,6]{3,2,1,0:T(1,128)} %param.5) | copy-start | bytes 292
  8.7 273.2 %all-gather.7.cloned.1.call-start = ((), (), s32[]{:S(2)}) async-start(), calls=%async_computation.1 | async-start | bytes 20971520 | tf_op jit(solution)/shard_map/all_gather | solution.py:76
  85.7 12.2 %copy-start = (bf16[1,64,1,6,128,128]{5,4,1,3,2,0:T(8,128)(2,1)S(1)}, bf16[1,64,1,6,128,128]{5,4,1,3,2,0:T(8,128)(2,1)}, u32[]{:S(2)}) copy-start(bf16[1,64,1,6,128,128]{5,4,1,3,2,0:T(8,128)(2,1)} %all-gather.9.cloned.1.call-done) | copy-start | bytes 37748740
  91.8 6.0 %copy-start.1 = (bf16[64,128,128]{2,1,0:T(8,128)(2,1)S(1)}, bf16[64,128,128]{2,1,0:T(8,128)(2,1)}, u32[]{:S(2)}) copy-start(bf16[64,128,128]{2,1,0:T(8,128)(2,1)} %gather_fusion.1) | copy-start | bytes 6291460
  97.8 3.7 copy-start.2
  101.5 3.6 copy-start.3
  105.1 3.7 copy-start.4
  296.9 15.3 %slice-start = ((s8[12582912]{0:T(1024)(128)(4,1)}), s8[4194304]{0:T(1024)(128)(4,1)S(1)}, s32[]{:S(2)}) async-start(s8[12582912]{0:T(1024)(128)(4,1)} %bitcast.88), calls=%async_computation.3 | async-start | bytes 8388608
  296.9 15.3 %slice-start.1 = ((s8[12582912]{0:T(1024)(128)(4,1)}), s8[4194304]{0:T(1024)(128)(4,1)S(1)}, s32[]{:S(2)}) async-start(s8[12582912]{0:T(1024)(128)(4,1)} %bitcast.88), calls=%async_computation.4 | async-start | bytes 8388608
  303.2 9.0 %slice-start.2 = ((s8[12582912]{0:T(1024)(128)(4,1)}), s8[4194304]{0:T(1024)(128)(4,1)S(1)}, s32[]{:S(2)}) async-start(s8[12582912]{0:T(1024)(128)(4,1)} %bitcast.88), calls=%async_computation.5 | async-start | bytes 8388608
Sparse Core Ops, SparseCore 0:
  9.2 76.4 all-gather.8
  124.8 157.0 all-gather.6
